TPU v7x, 32 devices: a whole 2x2x4 slice. The times are simulated.
32 devices in a mesh: rep: 2 (over x), tp: 8 (over z, y), sub: 2 (over core).
Axes of the slice: x: 2, y: 2, z: 4, core: 2. Of those that a mesh axis runs over, the one named last changes fastest.
Arguments:
- attention: bfloat16 [1024, 8192], P('rep', ('tp', 'sub')), parts along dimension 0, may hold values from -6 to 6
- out_weight: bfloat16 [8192, 8192], P(('tp', 'sub')), may hold values from -0.09375 to 0.09375
- residual: bfloat16 [1024, 8192], P('rep', ('tp', 'sub')), parts along dimension 0, may hold values from -6 to 6
- norm_gain: bfloat16 [8192], P(('tp', 'sub')), may hold values from 0.25 to 1.75
Outputs:
- quantized: bfloat16 [1024, 8192], P('rep'), parts along dimension 0
- scales: bfloat16 [1024, 64], P('rep'), parts along dimension 0
- new_residual: bfloat16 [1024, 8192], P('rep', ('tp', 'sub')), parts along dimension 0
There are 2 independent parts, one for each index of `rep`. A program takes and returns all parts, laid end to end along the dimension named above; an argument that names none is the same for every part. Nothing has to cross between parts.
All inputs are finite; a program needn't handle non-finite values.
Results may differ from a plain program's by a relative error of at most 0.0048.
Values may be sent and summed in bfloat16 or wider, within the bound.
A program may use at most 128 MiB of HBM per device.

v0:
```python
import jax
import jax.numpy as jnp
from jax import lax
from jax.sharding import PartitionSpec as P

BLOCK = 128
epsilon = 0.1
floor_scale = 0.5


def per_device(attention, out_weight, residual, norm_gain):
    width_all = out_weight.shape[1]
    summed = lax.psum_scatter(
        lax.dot_general(
            out_weight, attention, (((0,), (1,)), ((), ())), preferred_element_type=jnp.float32
        ),
        ("tp", "sub"),
        scatter_dimension=0,
        tiled=True,
    )
    hidden = residual.astype(jnp.float32) + summed.T
    new_residual = hidden.astype(jnp.bfloat16)
    squares = lax.psum(jnp.sum(hidden * hidden, axis=1), ("tp", "sub"))
    mean_square = squares / width_all
    normed = hidden * lax.rsqrt(mean_square + epsilon)[:, None] * norm_gain.astype(jnp.float32)
    blocks = normed.reshape(hidden.shape[0], hidden.shape[1] // BLOCK, BLOCK)
    largest = jnp.max(jnp.abs(blocks), axis=2)
    scales = jnp.maximum(largest, floor_scale).astype(jnp.bfloat16)
    quantized = (
        (blocks / scales.astype(jnp.float32)[:, :, None]).reshape(hidden.shape).astype(jnp.bfloat16)
    )
    full_quant, full_scales = (
        lax.all_gather(quantized, ("tp", "sub"), axis=1, tiled=True),
        lax.all_gather(scales, ("tp", "sub"), axis=1, tiled=True),
    )
    return (full_quant, full_scales, new_residual)


def solution(mesh):
    in_specs = (
        P("rep", ("tp", "sub")),
        P(("tp", "sub"), None),
        P("rep", ("tp", "sub")),
        P(("tp", "sub")),
    )
    out_specs = (P("rep", None), P("rep", None), P("rep", ("tp", "sub")))
    return jax.shard_map(
        per_device, mesh=mesh, in_specs=in_specs, out_specs=out_specs, check_vma=False
    )
```

profile of v0, /device:TPU:0, one launch (start us, length us, event | category | flops | bytes accessed | tf_op | source)
XLA Modules:
  0.0 327.3 jit_solution(3654953643072817745)
XLA Ops:
  7.2 0.0 copy-start
  7.2 0.0 reduce-scatter.2.cloned.1.call-start
  7.2 1.0 copy-done
  8.2 11.7 %fusion.5 = f32[8192,512]{1,0:T(8,128)} fusion(bf16[512,8192]{1,0:T(8,128)(2,1)} %param.5, bf16[512,512]{1,0:T(8,128)(2,1)S(1)} %copy-done), kind=kOutput, calls=%fused_computation.12 | convolution fusion | flops 4294967296 | bytes 25690112 | tf_op jit(solution)/shard_map/dot_general | solution.py:14
  19.9 0.0 copy-start.1
  19.9 0.0 copy-start.2
  19.9 0.0 reduce-scatter.2.cloned.1.call-update
  19.9 0.0 all-gather.3.cloned.1.call-start
  20.0 1.0 copy-done.1
  20.9 0.2 copy.10
  21.2 0.0 copy-done.2
  21.2 179.0 %reduce-scatter.2.cloned.1.call-done = f32[512,512]{1,0:T(8,128)} async-done(((f32[8192,512]{1,0:T(8,128)}), f32[512,512]{1,0:T(8,128)}) %reduce-scatter.2.cloned.1.call-update) | async-done | bytes 1048592 | tf_op jit(solution)/shard_map/reduce_scatter | solution.py:13
  200.1 1.4 multiply_reduce_fusion
  201.5 31.5 %psum.7 = f32[512]{0:T(512)S(1)} all-reduce(f32[512]{0:T(512)S(1)} %multiply_reduce_fusion), channel_id=1, replica_groups=mesh['rep'=2,'tp'=8,'sub'=2] {'tp','sub'}, use_global_device_ids=true, to_apply=%region_2.0 | all-reduce | flops 512 | bytes 4096 | tf_op jit(solution)/shard_map/psum | solution.py:23
  233.1 1.4 bitcast_reduce_fusion
  234.5 2.2 fusion.2
  236.7 0.0 all-gather.3.cloned.1.call-update
  236.8 1.0 copy.12
  237.8 17.8 %all-gather = bf16[16,4,512]{2,1,0:T(4,128)(2,1)S(1)} all-gather(bf16[1,4,512]{2,1,0:T(4,128)(2,1)S(1)} %get-tuple-element.11), channel_id=1, replica_groups=mesh['rep'=2,'tp'=8,'sub'=2] {'tp','sub'}, dimensions={0}, use_global_device_ids=true | all-gather | bytes 69632 | tf_op jit(solution)/shard_map/all_gather | solution.py:34
  255.6 0.6 reshape.18
  256.2 52.3 %all-gather.3.cloned.1.call-done = bf16[512,8192]{0,1:T(8,128)(2,1)} async-done(((bf16[512,512]{0,1:T(8,128)(2,1)}), bf16[512,8192]{0,1:T(8,128)(2,1)}) %all-gather.3.cloned.1.call-update) | async-done | bytes 8388624 | tf_op jit(solution)/shard_map/all_gather | solution.py:33
  308.6 11.9 %copy.11 = bf16[512,8192]{1,0:T(8,128)(2,1)} copy(bf16[512,8192]{0,1:T(8,128)(2,1)} %all-gather.3.cloned.1.call-done) | data formatting | bytes 16777216
  (3 shorter events, 0.0 us)
Async XLA Ops:
  7.2 1.0 copy-start
  7.2 193.0 %reduce-scatter.2.cloned.1.call-start = ((), (), s32[]{:S(2)}) async-start(), calls=%async_computation.1 | async-start | bytes 17825792 | tf_op jit(solution)/shard_map/reduce_scatter | solution.py:13
  19.9 1.0 copy-start.1
  19.9 1.3 copy-start.2
  19.9 288.6 %all-gather.3.cloned.1.call-start = ((), (), s32[]{:S(2)}) async-start(), calls=%async_computation.2 | async-start | bytes 8912896 | tf_op jit(solution)/shard_map/all_gather | solution.py:33
Sparse Core Ops, SparseCore 0:
  20.0 180.0 reduce-scatter.1
  236.9 71.6 all-gather.2
where the time goes:
time: 328 us; the launch traced here: 327 us
  waiting for transfers between devices  231 us (70%)
  blocking collectives  49.3 us (15%)
  local copies, waits for them, and re-layouts  15.7 us (5%)
  between operations  14.1 us (4%)
  matrix products  11.7 us (4%)
  other arithmetic  5.1 us (2%)
    reduce_scatter x1, waiting for transfers between devices, per_device(): lax.psum_scatter(lax.dot_general(out_weight, attention, (((0,), (1,)), ((...  179 us
    all_gather x1, waiting for transfers between devices, per_device(): lax.all_gather(quantized, ('tp', 'sub'), axis=1, tiled=True)  52.3 us
    psum x1, blocking collectives, per_device(): squares = lax.psum(jnp.sum(hidden * hidden, axis=1), ('tp', 'sub'))  31.5 us
    all_gather x1, blocking collectives, per_device(): lax.all_gather(scales, ('tp', 'sub'), axis=1, tiled=True)  17.8 us
    unnamed x10, local copies, waits for them, and re-layouts  15.7 us
    dot_general x1, matrix products, per_device(): lax.dot_general(out_weight, attention, (((0,), (1,)), ((), ())), preferre...  11.7 us
  transfers between devices with their start and end apart: 2, of which 2 were waited for; matrix products, arithmetic and copies ran while one was open for 1% of the time, Pallas kernels for 0%

commit v1 on v0

--- a/solution.py
+++ b/solution.py
@@ -20,7 +20,7 @@
     )
     hidden = residual.astype(jnp.float32) + summed.T
     new_residual = hidden.astype(jnp.bfloat16)
-    squares = lax.psum(jnp.sum(hidden * hidden, axis=1), ("tp", "sub"))
+    squares = jnp.sum(lax.all_gather(jnp.sum(hidden * hidden, axis=1), ("tp", "sub")), axis=0)
     mean_square = squares / width_all
     normed = hidden * lax.rsqrt(mean_square + epsilon)[:, None] * norm_gain.astype(jnp.float32)
     blocks = normed.reshape(hidden.shape[0], hidden.shape[1] // BLOCK, BLOCK)

time: 328 us -> 316 us (0.963)
  blocking collectives: 49.3 us -> 37.6 us
    psum x1 -> x0, blocking collectives: 31.5 us -> none  [per_device(): squares = lax.psum(jnp.sum(hidden * hidden, axis=1), ('tp', 'sub'))]
    all_gather x0 -> x1, blocking collectives: none -> 19.5 us  [per_device(): lax.all_gather(jnp.sum(hidden * hidden, axis=1), ('tp', 'sub'))]
where the time goes in v1:
time: 316 us; the launch traced here: 315 us
  waiting for transfers between devices  231 us (73%)
  blocking collectives  37.6 us (12%)
  local copies, waits for them, and re-layouts  15.7 us (5%)
  between operations  14.1 us (4%)
  matrix products  11.7 us (4%)
  other arithmetic  5.14 us (2%)
    reduce_scatter x1, waiting for transfers between devices, per_device(): lax.psum_scatter(lax.dot_general(out_weight, attention, (((0,), (1,)), ((...  179 us
    all_gather x1, waiting for transfers between devices, per_device(): lax.all_gather(quantized, ('tp', 'sub'), axis=1, tiled=True)  52.1 us
    all_gather x1, blocking collectives, per_device(): lax.all_gather(jnp.sum(hidden * hidden, axis=1), ('tp', 'sub'))  19.5 us
    all_gather x1, blocking collectives, per_device(): lax.all_gather(scales, ('tp', 'sub'), axis=1, tiled=True)  18.1 us
    unnamed x10, local copies, waits for them, and re-layouts  15.7 us
    dot_general x1, matrix products, per_device(): lax.dot_general(out_weight, attention, (((0,), (1,)), ((), ())), preferre...  11.7 us
  transfers between devices with their start and end apart: 2, of which 2 were waited for; matrix products, arithmetic and copies ran while one was open for 1% of the time, Pallas kernels for 0%

profile of v1, /device:TPU:0, one launch (start us, length us, event | category | flops | bytes accessed | tf_op | source)
XLA Modules:
  0.0 315.4 jit_solution(3037648148425405760)
XLA Ops:
  7.2 0.0 copy-start
  7.2 0.0 reduce-scatter.2.cloned.1.call-start
  7.2 1.0 copy-done
  8.2 11.7 %fusion.5 = f32[8192,512]{1,0:T(8,128)} fusion(bf16[512,8192]{1,0:T(8,128)(2,1)} %param.5, bf16[512,512]{1,0:T(8,128)(2,1)S(1)} %copy-done), kind=kOutput, calls=%fused_computation.12 | convolution fusion | flops 4294967296 | bytes 25690112 | tf_op jit(solution)/shard_map/dot_general | solution.py:14
  19.9 0.0 copy-start.1
  19.9 0.0 copy-start.2
  19.9 0.0 reduce-scatter.2.cloned.1.call-update
  19.9 0.0 all-gather.5.cloned.1.call-start
  20.0 1.0 copy-done.1
  20.9 0.2 copy.10
  21.2 0.0 copy-done.2
  21.2 179.0 %reduce-scatter.2.cloned.1.call-done = f32[512,512]{1,0:T(8,128)} async-done(((f32[8192,512]{1,0:T(8,128)}), f32[512,512]{1,0:T(8,128)}) %reduce-scatter.2.cloned.1.call-update) | async-done | bytes 1048592 | tf_op jit(solution)/shard_map/reduce_scatter | solution.py:13
  200.1 1.4 multiply_reduce_fusion
  201.5 19.5 %all-gather.1 = f32[16,1,512]{2,1,0:T(1,128)S(1)} all-gather(f32[1,1,512]{2,1,0:T(1,128)S(1)} %bitcast.25), channel_id=2, replica_groups=mesh['rep'=2,'tp'=8,'sub'=2] {'tp','sub'}, dimensions={0}, use_global_device_ids=true | all-gather | bytes 34816 | tf_op jit(solution)/shard_map/all_gather | solution.py:23
  221.1 1.4 bitcast_reduce_fusion
  222.6 2.2 fusion.2
  224.8 0.0 all-gather.5.cloned.1.call-update
  224.8 1.0 copy.12
  225.8 18.1 %all-gather.2 = bf16[16,4,512]{2,1,0:T(4,128)(2,1)S(1)} all-gather(bf16[1,4,512]{2,1,0:T(4,128)(2,1)S(1)} %get-tuple-element.11), channel_id=1, replica_groups=mesh['rep'=2,'tp'=8,'sub'=2] {'tp','sub'}, dimensions={0}, use_global_device_ids=true | all-gather | bytes 69632 | tf_op jit(solution)/shard_map/all_gather | solution.py:34
  244.0 0.6 reshape.25
  244.6 52.1 %all-gather.5.cloned.1.call-done = bf16[512,8192]{0,1:T(8,128)(2,1)} async-done(((bf16[512,512]{0,1:T(8,128)(2,1)}), bf16[512,8192]{0,1:T(8,128)(2,1)}) %all-gather.5.cloned.1.call-update) | async-done | bytes 8388624 | tf_op jit(solution)/shard_map/all_gather | solution.py:33
  296.7 11.9 %copy.11 = bf16[512,8192]{1,0:T(8,128)(2,1)} copy(bf16[512,8192]{0,1:T(8,128)(2,1)} %all-gather.5.cloned.1.call-done) | data formatting | bytes 16777216
  (4 shorter events, 0.1 us)
Async XLA Ops:
  7.2 1.0 copy-start
  7.2 193.0 %reduce-scatter.2.cloned.1.call-start = ((), (), s32[]{:S(2)}) async-start(), calls=%async_computation.1 | async-start | bytes 17825792 | tf_op jit(solution)/shard_map/reduce_scatter | solution.py:13
  19.9 1.0 copy-start.1
  19.9 1.3 copy-start.2
  19.9 276.8 %all-gather.5.cloned.1.call-start = ((), (), s32[]{:S(2)}) async-start(), calls=%async_computation.2 | async-start | bytes 8912896 | tf_op jit(solution)/shard_map/all_gather | solution.py:33
Sparse Core Ops, SparseCore 0:
  20.0 180.0 reduce-scatter.1
  224.9 71.6 all-gather.4
